TPU v7x, 32 devices: a whole 2x2x4 slice. The times are simulated.
32 devices in a mesh: orient: 8 (over z, y), dom: 4 (over x, core).
Axes of the slice: x: 2, y: 2, z: 4, core: 2. Of those that a mesh axis runs over, the one named last changes fastest.
Arguments:
- particles: bfloat16 [256, 8448], P(('dom', 'orient')), parts along dimension 0, may hold values from -12 to 12
- defocus: float32 [256], P(('dom', 'orient')), parts along dimension 0, may hold values from 10 to 60
- inv_noise: float32 [4224], replicated, may hold values from 0.5 to 2
- references: bfloat16 [13824, 8448], P(('dom', 'orient')), parts along dimension 0, may hold values from -0.25 to 0.25
- thresholds: int32 [256], P('dom'), parts along dimension 0, may hold values from 512 to 1023
- range_start: int32 [256], P('dom'), parts along dimension 0, may hold values from 0 to 3455
- range_len: int32 [256], P('dom'), parts along dimension 0, may hold values from 36 to 1727
Outputs:
- posterior: float32 [256, 3456], P('dom', 'orient'), parts along dimension 0
- cumulative: float32 [256, 3456], P('dom', 'orient'), parts along dimension 0
- log_evidence: float32 [256], P('dom'), parts along dimension 0
- kept_mass: float32 [256], P('dom'), parts along dimension 0
There are 4 independent parts, one for each index of `dom`. A program takes and returns all parts, laid end to end along the dimension named above; an argument that names none is the same for every part. Nothing has to cross between parts.
All inputs are finite; a program needn't handle non-finite values.
Results may differ from a plain program's by a relative error of at most 0.0004.
The roundings to bfloat16 on the way count: a program that leaves them out, or rounds other values in their place, can miss the bound.
Values may be sent and summed in bfloat16 or wider, within the bound.
A program may use at most 64 MiB of HBM per device.

v0:
```python
import math
import jax
import jax.numpy as jnp
from jax import lax
from jax.sharding import PartitionSpec as P


def ctf_table(defocus, coef):
    index = jnp.arange(coef, dtype=jnp.int32)
    row_pos = (index // 128).astype(jnp.float32)
    col_pos = (index % 128 - 64).astype(jnp.float32)
    freq = math.pi * (row_pos * row_pos + col_pos * col_pos) / 16384.0
    return -jnp.sin(defocus[:, None] * freq[None, :] + 0.07)


def on_device(particles, defocus, inv_noise, references, thresholds, range_start, range_len):
    coef = inv_noise.shape[0]
    feat = 2 * coef
    ori_dev = references.shape[0]
    ctf = ctf_table(defocus, coef)
    ctf_both = jnp.concatenate([ctf, ctf], axis=1)
    noise_both = jnp.concatenate([inv_noise, inv_noise])
    weighted = (particles.astype(jnp.float32) * ctf_both * noise_both[None, :]).astype(jnp.bfloat16)
    ctf_power = (ctf * ctf * inv_noise[None, :]).astype(jnp.bfloat16)
    packed = jnp.concatenate([weighted, ctf_power], axis=1)
    real_part = references[:, :coef].astype(jnp.float32)
    imag_part = references[:, coef:].astype(jnp.float32)
    power = (real_part * real_part + imag_part * imag_part).astype(jnp.bfloat16)
    dims = (((1,), (1,)), ((), ()))
    piece = lax.all_gather(packed, "orient", axis=0, tiled=True)
    cross = lax.dot_general(piece[:, :feat], references, dims, preferred_element_type=jnp.float32)
    energy = lax.dot_general(piece[:, feat:], power, dims, preferred_element_type=jnp.float32)
    scores = cross - 0.5 * energy
    local_top = jnp.max(scores, axis=1)
    local_sum = jnp.sum(jnp.exp(scores - local_top[:, None]), axis=1)
    all_tops, all_sums = (
        lax.all_gather(local_top[None, :], "orient", axis=0, tiled=True),
        lax.all_gather(local_sum[None, :], "orient", axis=0, tiled=True),
    )
    top_score = jnp.max(all_tops, axis=0)
    scaled = all_sums * jnp.exp(all_tops - top_score[None, :])
    total = jnp.sum(scaled, axis=0)
    ranks = jnp.arange(all_tops.shape[0], dtype=jnp.int32)
    earlier_rows = (ranks < lax.axis_index("orient"))[:, None]
    shifted = jnp.sum(jnp.where(earlier_rows, scaled, 0.0), axis=0)
    expon = jnp.exp(scores - top_score[:, None])
    posterior = expon / total[:, None]
    row_ids = lax.broadcasted_iota(jnp.int32, (ori_dev, ori_dev), 0)
    col_ids = lax.broadcasted_iota(jnp.int32, (ori_dev, ori_dev), 1)
    upper = (row_ids <= col_ids).astype(jnp.float32)
    running = jnp.dot(
        expon, upper, precision=lax.Precision.HIGHEST, preferred_element_type=jnp.float32
    )
    cumulative = (shifted[:, None] + running) / total[:, None]
    before = cumulative - posterior
    fraction = thresholds.astype(jnp.float32) / 1024.0
    kept = jnp.minimum(jnp.maximum(fraction[:, None] - before, 0.0), posterior)
    all_orients = lax.axis_size("orient") * ori_dev
    orient_ids = lax.axis_index("orient") * ori_dev + jnp.arange(ori_dev, dtype=jnp.int32)
    inside = (orient_ids[None, :] - range_start[:, None]) % all_orients < range_len[:, None]
    local_kept = jnp.sum(jnp.where(inside, kept, 0.0), axis=1)
    kept_mass = lax.psum(local_kept, "orient")
    log_evidence = top_score + jnp.log(total)
    return (posterior, cumulative, log_evidence, kept_mass)


def solution(mesh):
    return jax.shard_map(
        on_device,
        mesh=mesh,
        in_specs=(
            P(("dom", "orient"), None),
            P(("dom", "orient")),
            P(),
            P(("dom", "orient"), None),
            P("dom"),
            P("dom"),
            P("dom"),
        ),
        out_specs=(P("dom", "orient"), P("dom", "orient"), P("dom"), P("dom")),
        check_vma=False,
    )
```

profile of v0, /device:TPU:0, one launch (start us, length us, event | category | flops | bytes accessed | tf_op | source)
XLA Modules:
  0.0 113.0 jit_solution(12283271416409016182)
XLA Ops:
  7.2 0.0 all-gather.4.cloned.1.call-start
  7.2 0.8 pad_maximum_fusion.1
  8.0 1.3 %fusion.7 = (f32[8,4224]{1,0:T(8,128)S(1)}, bf16[8,4224]{1,0:T(8,128)(2,1)S(1)}) fusion(f32[4224]{0:T(1024)S(1)} %fusion.23, f32[8]{0:T(128)} %param.8, f32[4224]{0:T(1024)} %param.9), kind=kLoop, calls=%fused_computation.16 | loop fusion | flops 202752 | bytes 236576 | tf_op jit(solution)/shard_map/neg | solution.py:13
  9.3 1.0 fusion.6
  10.3 0.7 pad_maximum_fusion
  11.0 0.0 all-gather.4.cloned.1.call-update
  11.0 1.2 %dynamic-slice = u32[1]{0:T(128)} dynamic-slice(u32[32]{0:T(128)} %constant.75, u32[]{:T(128)S(6)} %add.76), dynamic_slice_sizes={1} | dynamic-slice | bytes 12
  12.9 0.7 convert_multiply_fusion
  13.6 45.1 %all-gather.4.cloned.1.call-done = bf16[64,12672]{1,0:T(8,128)(2,1)} async-done(((bf16[8,12672]{1,0:T(8,128)(2,1)}), bf16[64,12672]{1,0:T(8,128)(2,1)}) %all-gather.4.cloned.1.call-update) | async-done | bytes 1622032 | tf_op jit(solution)/shard_map/all_gather | solution.py:30
  58.6 0.0 copy-start
  58.7 0.0 copy-start.1
  58.7 5.0 %fusion.2 = f32[64,432]{1,0:T(8,128)S(1)} fusion(bf16[432,8448]{1,0:T(8,128)(2,1)} %param.10, bf16[64,12672]{1,0:T(8,128)(2,1)} %all-gather.4.cloned.1.call-done), kind=kOutput, calls=%fused_computation.5 | convolution fusion | flops 244546560 | bytes 7950336 | tf_op jit(solution)/shard_map/dot_general | solution.py:32
  63.6 0.4 copy-done
  64.0 0.4 copy-done.1
  64.4 0.0 copy-start.2
  64.4 0.0 copy-start.3
  64.5 2.3 %fusion.30 = (f32[64]{0:T(128)S(1)}, f32[64,432]{1,0:T(8,128)S(1)}) fusion(f32[64,432]{1,0:T(8,128)S(1)} %fusion.2, bf16[432,8448]{1,0:T(8,128)(2,1)S(1)} %copy-done, bf16[64,12672]{1,0:T(8,128)(2,1)S(1)} %copy-done.1), kind=kOutput, calls=%fused_computation.53 | convolution fusion | flops 467195840 | bytes 8622336 | tf_op jit(solution)/shard_map/dot_general | solution.py:31
  66.8 0.2 exponential_reduce_fusion
  67.0 0.2 dynamic-update-slice
  67.2 0.2 dynamic-update-slice.1
  67.4 18.8 %all-reduce.2 = (f32[512]{0:T(512)S(1)}, f32[512]{0:T(512)S(1)}) all-reduce(f32[512]{0:T(512)S(1)} %dynamic-update-slice.1, f32[512]{0:T(512)S(1)} %dynamic-update-slice), channel_id=3, replica_groups=mesh['orient'=8,'dom'=4] {'orient'}, use_global_device_ids=true, to_apply=%add.1 | all-reduce | flops 1024 | bytes 8192
  86.2 0.1 reshape.54
  86.3 0.1 reshape.55
  86.4 0.1 select_reduce_fusion.1
  86.4 0.5 log_add_fusion
  87.0 0.0 copy-done.2
  87.0 0.0 copy-done.3
  87.0 1.2 %select_reduce_fusion = (f32[64]{0:T(128)S(1)}, f32[64,432]{1,0:T(8,128)}, f32[64,432]{1,0:T(8,128)}) fusion(f32[64]{0:T(128)S(1)} %convert_multiply_fusion, s32[64]{0:T(128)S(1)} %copy-done.2, s32[64]{0:T(128)S(1)} %copy-done.3, s32[432]{0:T(512)S(1)} %iota_add_fusion, f32[64]{0:T(128)S(1)} %get-tuple-element.5, f32[64,432]{1,0:T(8,128)S(1)} %get-tuple-element.13, ...), kind=kOutput, calls=%fused_computation.18 | convolution fusion | flops 144039104 | bytes 335296 | tf_op jit(solution)/shard_map/dot_general | solution.py:51
  88.1 18.0 %psum.7 = f32[64]{0:T(128)} all-reduce(f32[64]{0:T(128)S(1)} %get-tuple-element.8), channel_id=1, replica_groups=mesh['orient'=8,'dom'=4] {'orient'}, use_global_device_ids=true, to_apply=%region_6.7 | all-reduce | flops 64 | bytes 512 | tf_op jit(solution)/shard_map/psum | solution.py:62
  (6 shorter events, 0.0 us)
Async XLA Ops:
  7.2 51.5 %all-gather.4.cloned.1.call-start = ((), (), s32[]{:S(2)}) async-start(), calls=%async_computation | async-start | bytes 1824768 | tf_op jit(solution)/shard_map/all_gather | solution.py:30
  58.6 5.4 %copy-start = (bf16[432,8448]{1,0:T(8,128)(2,1)S(1)}, bf16[432,8448]{1,0:T(8,128)(2,1)}, u32[]{:S(2)}) copy-start(bf16[432,8448]{1,0:T(8,128)(2,1)} %param.10) | copy-start | bytes 21897220
  58.7 5.8 %copy-start.1 = (bf16[64,12672]{1,0:T(8,128)(2,1)S(1)}, bf16[64,12672]{1,0:T(8,128)(2,1)}, u32[]{:S(2)}) copy-start(bf16[64,12672]{1,0:T(8,128)(2,1)} %all-gather.4.cloned.1.call-done) | copy-start | bytes 4866052
  64.4 22.5 %copy-start.2 = (s32[64]{0:T(128)S(1)}, s32[64]{0:T(128)}, u32[]{:S(2)}) copy-start(s32[64]{0:T(128)} %param.13) | copy-start | bytes 772
  64.4 22.5 %copy-start.3 = (s32[64]{0:T(128)S(1)}, s32[64]{0:T(128)}, u32[]{:S(2)}) copy-start(s32[64]{0:T(128)} %param.12) | copy-start | bytes 772
Sparse Core Ops, SparseCore 0:
  11.1 47.4 all-gather.3
where the time goes:
time: 113 us
  waiting for transfers between devices  45.1 us (40%)
  blocking collectives  36.7 us (32%)
  between operations  14.7 us (13%)
  matrix products  8.47 us (7%)
  other arithmetic  5.25 us (5%)
  local copies, waits for them, and re-layouts  2.66 us (2%)
    all_gather x1, waiting for transfers between devices, on_device(): piece = lax.all_gather(packed, 'orient', axis=0, tiled=True)  45.1 us
    unnamed x1, blocking collectives  18.8 us
    psum x1, blocking collectives, on_device(): kept_mass = lax.psum(local_kept, 'orient')  18 us
    dot_general x1, matrix products, on_device(): lax.dot_general(piece[:, feat:], power, dims, preferred_element_type=jnp....  4.98 us
    unnamed x13, local copies, waits for them, and re-layouts  2.51 us
    dot_general x1, matrix products, on_device(): lax.dot_general(piece[:, :feat], references, dims, preferred_element_type...  2.33 us
  transfers between devices with their start and end apart: 1, of which 1 were waited for; matrix products, arithmetic and copies ran while one was open for 2% of the time, Pallas kernels for 0%

commit v1 on v0

--- a/solution.py
+++ b/solution.py
@@ -3,6 +3,15 @@
 import jax.numpy as jnp
 from jax import lax
 from jax.sharding import PartitionSpec as P
+
+
+def spread_wires(obj, across):
+    n_lanes = lax.axis_size(across)
+    inter = obj
+    v_next = lambda parts_out: [(w, w ^ parts_out) for w in range(n_lanes)]
+    for h in range(n_lanes.bit_length() - 1):
+        inter = inter + lax.ppermute(inter, axis_name=across, perm=v_next(1 << h))
+    return inter
 
 
 def ctf_table(defocus, coef):
@@ -59,7 +68,7 @@
     orient_ids = lax.axis_index("orient") * ori_dev + jnp.arange(ori_dev, dtype=jnp.int32)
     inside = (orient_ids[None, :] - range_start[:, None]) % all_orients < range_len[:, None]
     local_kept = jnp.sum(jnp.where(inside, kept, 0.0), axis=1)
-    kept_mass = lax.psum(local_kept, "orient")
+    kept_mass = spread_wires(local_kept, "orient")
     log_evidence = top_score + jnp.log(total)
     return (posterior, cumulative, log_evidence, kept_mass)
 

time: 113 us -> 107 us (0.947)
  blocking collectives: 36.7 us -> 18.8 us
  waiting for transfers between devices: 45.1 us -> 55.8 us
    psum x1 -> x0, blocking collectives: 18 us -> none  [on_device(): kept_mass = lax.psum(local_kept, 'orient')]
    ppermute x0 -> x3, waiting for transfers between devices: none -> 10.7 us  [spread_wires(): inter = inter + lax.ppermute(inter, axis_name=across, perm=v_next(1 << h))]
  transfers between devices with their start and end apart: 1 -> 4, of which waited for: 1 -> 4; matrix products, arithmetic and copies ran while one was open for 2% -> 2% of each run, Pallas kernels for 0% -> 0%
where the time goes in v1:
time: 107 us
  waiting for transfers between devices  55.8 us (52%)
  blocking collectives  18.8 us (18%)
  between operations  14.8 us (14%)
  matrix products  8.47 us (8%)
  other arithmetic  5.77 us (5%)
  local copies, waits for them, and re-layouts  2.66 us (2%)
    all_gather x1, waiting for transfers between devices, on_device(): piece = lax.all_gather(packed, 'orient', axis=0, tiled=True)  45.1 us
    unnamed x1, blocking collectives  18.8 us
    ppermute x3, waiting for transfers between devices, spread_wires(): inter = inter + lax.ppermute(inter, axis_name=across, perm=v_next(1 << h))  10.7 us
    dot_general x1, matrix products, on_device(): lax.dot_general(piece[:, feat:], power, dims, preferred_element_type=jnp....  4.98 us
    unnamed x13, local copies, waits for them, and re-layouts  2.51 us
    dot_general x1, matrix products, on_device(): lax.dot_general(piece[:, :feat], references, dims, preferred_element_type...  2.33 us
  transfers between devices with their start and end apart: 4, of which 4 were waited for; matrix products, arithmetic and copies ran while one was open for 2% of the time, Pallas kernels for 0%

profile of v1, /device:TPU:0, one launch (start us, length us, event | category | flops | bytes accessed | tf_op | source)
XLA Modules:
  0.0 106.7 jit_solution(2375181934518018125)
XLA Ops:
  7.2 0.0 all-gather.4.cloned.1.call-start
  7.2 0.8 pad_maximum_fusion.1
  8.0 1.3 %fusion.7 = (f32[8,4224]{1,0:T(8,128)S(1)}, bf16[8,4224]{1,0:T(8,128)(2,1)S(1)}) fusion(f32[4224]{0:T(1024)S(1)} %fusion.23, f32[8]{0:T(128)} %param.8, f32[4224]{0:T(1024)} %param.9), kind=kLoop, calls=%fused_computation.16 | loop fusion | flops 202752 | bytes 236576 | tf_op jit(solution)/shard_map/neg | solution.py:22
  9.3 1.0 fusion.6
  10.3 0.7 pad_maximum_fusion
  11.0 0.0 all-gather.4.cloned.1.call-update
  11.0 1.2 %dynamic-slice = u32[1]{0:T(128)} dynamic-slice(u32[32]{0:T(128)} %constant.75, u32[]{:T(128)S(6)} %add.86), dynamic_slice_sizes={1} | dynamic-slice | bytes 12
  12.9 0.7 convert_multiply_fusion
  13.6 45.1 %all-gather.4.cloned.1.call-done = bf16[64,12672]{1,0:T(8,128)(2,1)} async-done(((bf16[8,12672]{1,0:T(8,128)(2,1)}), bf16[64,12672]{1,0:T(8,128)(2,1)}) %all-gather.4.cloned.1.call-update) | async-done | bytes 1622032 | tf_op jit(solution)/shard_map/all_gather | solution.py:39
  58.6 0.0 copy-start
  58.7 0.0 copy-start.1
  58.7 5.0 %fusion.2 = f32[64,432]{1,0:T(8,128)S(1)} fusion(bf16[432,8448]{1,0:T(8,128)(2,1)} %param.10, bf16[64,12672]{1,0:T(8,128)(2,1)} %all-gather.4.cloned.1.call-done), kind=kOutput, calls=%fused_computation.5 | convolution fusion | flops 244546560 | bytes 7950336 | tf_op jit(solution)/shard_map/dot_general | solution.py:41
  63.6 0.4 copy-done
  64.0 0.4 copy-done.1
  64.4 0.0 copy-start.2
  64.4 0.0 copy-start.3
  64.5 2.3 %fusion.30 = (f32[64]{0:T(128)S(1)}, f32[64,432]{1,0:T(8,128)S(1)}) fusion(f32[64,432]{1,0:T(8,128)S(1)} %fusion.2, bf16[432,8448]{1,0:T(8,128)(2,1)S(1)} %copy-done, bf16[64,12672]{1,0:T(8,128)(2,1)S(1)} %copy-done.1), kind=kOutput, calls=%fused_computation.53 | convolution fusion | flops 467195840 | bytes 8622336 | tf_op jit(solution)/shard_map/dot_general | solution.py:40
  66.8 0.2 exponential_reduce_fusion
  67.0 0.2 dynamic-update-slice
  67.2 0.2 dynamic-update-slice.1
  67.4 18.8 %all-reduce.2 = (f32[512]{0:T(512)S(1)}, f32[512]{0:T(512)S(1)}) all-reduce(f32[512]{0:T(512)S(1)} %dynamic-update-slice.1, f32[512]{0:T(512)S(1)} %dynamic-update-slice), channel_id=3, replica_groups=mesh['orient'=8,'dom'=4] {'orient'}, use_global_device_ids=true, to_apply=%add.1 | all-reduce | flops 1024 | bytes 8192
  86.2 0.1 reshape.54
  86.3 0.1 reshape.55
  86.4 0.1 select_reduce_fusion.1
  86.4 0.0 copy-done.2
  86.5 0.0 copy-done.3
  86.5 1.2 %select_reduce_fusion = (f32[64]{0:T(128)S(1)}, f32[64,432]{1,0:T(8,128)}, f32[64,432]{1,0:T(8,128)}) fusion(f32[64]{0:T(128)S(1)} %convert_multiply_fusion, s32[64]{0:T(128)S(1)} %copy-done.2, s32[64]{0:T(128)S(1)} %copy-done.3, s32[432]{0:T(512)S(1)} %iota_add_fusion, f32[64]{0:T(128)S(1)} %get-tuple-element.5, f32[64,432]{1,0:T(8,128)S(1)} %get-tuple-element.13, ...), kind=kOutput, calls=%fused_computation.18 | convolution fusion | flops 144039104 | bytes 335296 | tf_op jit(solution)/shard_map/dot_general | solution.py:60
  87.6 0.4 collective-permute-start
  88.1 3.2 %collective-permute-done = f32[64]{0:T(128)S(1)} collective-permute-done((f32[64]{0:T(128)S(1)}, f32[64]{0:T(128)S(1)}, u32[]{:S(2)}, u32[]{:S(2)}) %collective-permute-start) | collective-permute-done | bytes 288 | tf_op jit(solution)/shard_map/ppermute | solution.py:13
  91.3 0.0 collective-permute-start.1
  91.3 3.6 %collective-permute-done.1 = f32[64]{0:T(128)S(1)} collective-permute-done((f32[64]{0:T(128)S(1)}, f32[64]{0:T(128)S(1)}, u32[]{:S(2)}, u32[]{:S(2)}) %collective-permute-start.1) | collective-permute-done | bytes 288 | tf_op jit(solution)/shard_map/ppermute | solution.py:13
  94.8 0.0 collective-permute-start.2
  94.8 0.5 log_add_fusion
  95.4 3.9 %collective-permute-done.2 = f32[64]{0:T(128)S(1)} collective-permute-done((f32[64]{0:T(128)S(1)}, f32[64]{0:T(128)S(1)}, u32[]{:S(2)}, u32[]{:S(2)}) %collective-permute-start.2) | collective-permute-done | bytes 288 | tf_op jit(solution)/shard_map/ppermute | solution.py:13
  99.3 0.5 add.85
  (8 shorter events, 0.0 us)
Async XLA Ops:
  7.2 51.5 %all-gather.4.cloned.1.call-start = ((), (), s32[]{:S(2)}) async-start(), calls=%async_computation | async-start | bytes 1824768 | tf_op jit(solution)/shard_map/all_gather | solution.py:39
  58.6 5.4 %copy-start = (bf16[432,8448]{1,0:T(8,128)(2,1)S(1)}, bf16[432,8448]{1,0:T(8,128)(2,1)}, u32[]{:S(2)}) copy-start(bf16[432,8448]{1,0:T(8,128)(2,1)} %param.10) | copy-start | bytes 21897220
  58.7 5.8 %copy-start.1 = (bf16[64,12672]{1,0:T(8,128)(2,1)S(1)}, bf16[64,12672]{1,0:T(8,128)(2,1)}, u32[]{:S(2)}) copy-start(bf16[64,12672]{1,0:T(8,128)(2,1)} %all-gather.4.cloned.1.call-done) | copy-start | bytes 4866052
  64.4 22.0 %copy-start.2 = (s32[64]{0:T(128)S(1)}, s32[64]{0:T(128)}, u32[]{:S(2)}) copy-start(s32[64]{0:T(128)} %param.13) | copy-start | bytes 772
  64.4 22.0 %copy-start.3 = (s32[64]{0:T(128)S(1)}, s32[64]{0:T(128)}, u32[]{:S(2)}) copy-start(s32[64]{0:T(128)} %param.12) | copy-start | bytes 772
  87.6 3.6 %collective-permute-start = (f32[64]{0:T(128)S(1)}, f32[64]{0:T(128)S(1)}, u32[]{:S(2)}, u32[]{:S(2)}) collective-permute-start(f32[64]{0:T(128)S(1)} %get-tuple-element.8), channel_id=1, source_target_pairs={{0,4},{4,0},{8,12},{12,8},{16,20},{20,16},{24,28},{28,24},{1,5},{5... | collective-permute-start | bytes 776 | tf_op jit(solution)/shard_map/ppermute | solution.py:13
  91.3 3.6 %collective-permute-start.1 = (f32[64]{0:T(128)S(1)}, f32[64]{0:T(128)S(1)}, u32[]{:S(2)}, u32[]{:S(2)}) collective-permute-start(f32[64]{0:T(128)S(1)} %add.83), channel_id=1, source_target_pairs={{0,8},{4,12},{8,0},{12,4},{16,24},{20,28},{24,16},{28,20},{1,9},{5... | collective-permute-start | bytes 776 | tf_op jit(solution)/shard_map/ppermute | solution.py:13
  94.8 4.5 %collective-permute-start.2 = (f32[64]{0:T(128)S(1)}, f32[64]{0:T(128)S(1)}, u32[]{:S(2)}, u32[]{:S(2)}) collective-permute-start(f32[64]{0:T(128)S(1)} %add.84), channel_id=1, source_target_pairs={{0,16},{4,20},{8,24},{12,28},{16,0},{20,4},{24,8},{28,12},{1,17},{... | collective-permute-start | bytes 776 | tf_op jit(solution)/shard_map/ppermute | solution.py:13
Sparse Core Ops, SparseCore 0:
  11.1 47.4 all-gather.3
